TPU v7x, 32 devices: a whole 2x2x4 slice. The times are simulated.
32 devices in a mesh: row: 8 (over y, x, core), col: 4 (over z).
Axes of the slice: x: 2, y: 2, z: 4, core: 2. Of those that a mesh axis runs over, the one named last changes fastest.
Arguments:
- tokens: bfloat16 [1024, 8192], P('row', 'col'), may hold values from -6 to 6
- weights: bfloat16 [2, 14336, 8192], P(None, 'row', 'col'), may hold values from -0.0625 to 0.0625
- gradients: bfloat16 [2, 14336, 8192], P(None, 'row', 'col'), may hold values from -200 to 200, as said below
- row_factors: float32 [2, 14336], P(None, 'row'), may hold values from 0.05 to 0.5
- col_factors: float32 [2, 8192], P(None, 'col'), may hold values from 0.05 to 0.5
Outputs:
- hidden: bfloat16 [1024, 14336], P('col', 'row')
- row_new: float32 [2, 14336], P(None, 'row')
- col_new: float32 [2, 8192], P(None, 'col')
Inputs may be any that keep to these rules, and one draw needn't show every extreme that they name: Finite real gradients.
All inputs are finite; a program needn't handle non-finite values.
Results may differ from a plain program's by a relative error of at most 0.001.
The roundings to bfloat16 on the way count: a program that leaves them out, or rounds other values in their place, can miss the bound.
Values may be sent and summed in bfloat16 or wider, within the bound.
No kernel may reach another device: no remote copies, remote signals or barrier semaphores. Data moves between devices by JAX's collectives and lax.ppermute only.
A program may use at most 128 MiB of HBM per device.

v0:
```python
import jax
import jax.numpy as jnp
from jax import lax
from jax.sharding import PartitionSpec as P

D = 8192
FF = 14336
decay_rate = 0.5
learn_rate = 0.01
clip_limit = 1.0
tiny_eps = 1e-30


def local(tokens, weights, gradients, row_factors, col_factors):
    gradient = gradients.astype(jnp.float32)
    squares = gradient * gradient
    row_part = jnp.sum(squares, axis=2)
    col_part = jnp.sum(squares, axis=1)
    row_block = row_part.shape[1]
    col_block = col_part.shape[1]
    row_total = lax.psum(row_part, "col")
    col_total = lax.psum(col_part, "row")
    row_new = decay_rate * row_factors + (1.0 - decay_rate) * (row_total / D + tiny_eps)
    col_new = decay_rate * col_factors + (1.0 - decay_rate) * (col_total / FF + tiny_eps)
    row_mean = lax.psum(jnp.sum(row_new, axis=1), "row") / FF
    denominator = jnp.sqrt(row_new[:, :, None] * col_new[:, None, :] / row_mean[:, None, None])
    update = gradient / denominator
    norm_total = lax.psum(jnp.sum(update * update, axis=(1, 2)), ("row", "col"))
    clip_scale = jnp.maximum(1.0, jnp.sqrt(norm_total / (FF * D)) / clip_limit)
    new_weights = (
        weights.astype(jnp.float32) - learn_rate * update / clip_scale[:, None, None]
    ).astype(jnp.bfloat16)
    spread = lax.all_gather(tokens, "row", axis=0, tiled=True)
    flat_weights = new_weights.reshape(2 * row_block, col_block)
    combined = lax.psum_scatter(
        lax.dot_general(
            spread, flat_weights, (((1,), (1,)), ((), ())), preferred_element_type=jnp.float32
        ),
        "col",
        scatter_dimension=0,
        tiled=True,
    )
    gate_proj = combined[:, :row_block]
    up_proj = combined[:, row_block:]
    hidden = (jax.nn.silu(gate_proj) * up_proj).astype(jnp.bfloat16)
    return (hidden, row_new, col_new)


def solution(mesh):
    placed = (
        P("row", "col"),
        P(None, "row", "col"),
        P(None, "row", "col"),
        P(None, "row"),
        P(None, "col"),
    )
    return jax.shard_map(
        local,
        mesh=mesh,
        in_specs=placed,
        out_specs=(P("col", "row"), P(None, "row"), P(None, "col")),
        check_vma=False,
    )
```

profile of v0, /device:TPU:0, one launch (start us, length us, event | category | flops | bytes accessed | tf_op | source)
XLA Modules:
  0.0 409.2 jit_solution(4668442278646132492)
XLA Ops:
  7.2 0.0 copy-start.3
  7.2 0.0 copy-start.2
  7.2 0.0 all-gather.2.cloned.1.call-start
  7.2 9.1 %fusion = (f32[2,2048]{1,0:T(2,128)S(1)}, f32[2,1792]{1,0:T(2,128)S(1)}) fusion(bf16[2,1792,2048]{2,1,0:T(8,128)(2,1)} %param.7), kind=kLoop, calls=%fused_computation.2 | loop fusion | flops 29352448 | bytes 14710784 | tf_op jit(solution)/shard_map/reduce_sum | solution.py:18
  16.4 20.5 %psum.28 = f32[2,1792]{1,0:T(2,128)S(1)} all-reduce(f32[2,1792]{1,0:T(2,128)S(1)} %get-tuple-element.7), channel_id=1, replica_groups=mesh['row'=8,'col'=4] {'col'}, use_global_device_ids=true, to_apply=%region_1.0 | all-reduce | flops 3584 | bytes 28672 | tf_op jit(solution)/shard_map/psum | solution.py:21
  36.9 0.0 copy-done.3
  36.9 0.1 fusion.3
  37.0 0.0 copy-start.1
  37.0 22.3 %all-reduce = (f32[2]{0:T(128)S(1)}, f32[2,2048]{1,0:T(2,128)S(1)}) all-reduce(f32[2]{0:T(128)S(1)} %get-tuple-element.10, f32[2,2048]{1,0:T(2,128)S(1)} %get-tuple-element.6), channel_id=1, replica_groups=mesh['row'=8,'col'=4] {'row'}, use_global_device_ids=true, to_apply=%region_5.0 | all-reduce | flops 4098 | bytes 32784 | tf_op jit(solution)/shard_map/psum | solution.py:25
  59.4 0.0 copy-done.2
  59.4 0.0 copy-start
  59.4 11.5 %multiply_reduce_fusion = f32[2]{0:T(128)S(1)} fusion(f32[2]{0:T(128)S(1)} %broadcast_multiply_fusion, f32[2,2048]{1,0:T(2,128)S(1)} %add_multiply_fusion, f32[2,1792]{1,0:T(2,128)S(1)} %get-tuple-element.11, bf16[2,1792,2048]{2,1,0:T(8,128)(2,1)} %param.7), kind=kLoop, calls=%fused_computation.5 | loop fusion | flops 44040192 | bytes 14710800 | tf_op jit(solution)/shard_map/reduce_sum | solution.py:28
  70.9 0.0 all-gather.2.cloned.1.call-update
  71.0 0.0 reduce-scatter.2.cloned.1.call-start
  71.0 37.5 %psum.31 = f32[2]{0:T(128)S(1)} all-reduce(f32[2]{0:T(128)S(1)} %multiply_reduce_fusion), channel_id=1, replica_groups=mesh['row'=8,'col'=4] {'row','col'}, use_global_device_ids=true, to_apply=%region_7.0 | all-reduce | flops 2 | bytes 16 | tf_op jit(solution)/shard_map/psum | solution.py:28
  108.6 20.8 %subtract_convert_fusion = bf16[2,1792,2048]{2,1,0:T(8,128)(2,1)} fusion(bf16[2,1792,2048]{2,1,0:T(8,128)(2,1)} %param.6, f32[2]{0:T(128)S(1)} %sqrt_maximum_fusion, f32[2]{0:T(128)S(1)} %broadcast_multiply_fusion, f32[2,2048]{1,0:T(2,128)S(1)} %add_multiply_fusion, f32[2,1792]{1,0:T(2,128)S(1)} %get-tuple-element.11, bf16[2,1792,2048]{2,1,0:T(8,128)(2,1)} %param.7), kind=kLoop, calls=%fused_computation.4 | loop fusion | flops 66060288 | bytes 44070928 | tf_op jit(solution)/shard_map/convert_element_type | solution.py:32
  129.3 0.0 copy-done.1
  129.3 0.0 copy-done
  129.3 0.0 all-gather.2.cloned.1.call-done
  129.4 21.9 %convolution_bitcast_fusion = f32[1024,3584]{0,1:T(8,128)} fusion(bf16[3584,2048]{1,0:T(8,128)(2,1)} %bitcast.5, bf16[1024,2048]{1,0:T(8,128)(2,1)} %all-gather.2.cloned.1.call-done), kind=kOutput, calls=%fused_computation.6 | convolution fusion | flops 15032385536 | bytes 33554432 | tf_op jit(solution)/shard_map/dot_general | solution.py:36
  151.3 0.0 reduce-scatter.2.cloned.1.call-update
  151.3 247.1 %reduce-scatter.2.cloned.1.call-done = f32[256,3584]{0,1:T(8,128)} async-done(((f32[1024,3584]{0,1:T(8,128)}), f32[256,3584]{0,1:T(8,128)}) %reduce-scatter.2.cloned.1.call-update) | async-done | bytes 3670032 | tf_op jit(solution)/shard_map/reduce_scatter | solution.py:35
  398.4 2.6 fusion.2
  401.0 1.4 copy.8
  (3 shorter events, 0.0 us)
Async XLA Ops:
  7.2 29.7 %copy-start.3 = (f32[2,1792]{1,0:T(2,128)S(1)}, f32[2,1792]{1,0:T(2,128)}, u32[]{:S(2)}) copy-start(f32[2,1792]{1,0:T(2,128)} %param.8) | copy-start | bytes 43012
  7.2 52.2 %copy-start.2 = (f32[2,2048]{1,0:T(2,128)S(1)}, f32[2,2048]{1,0:T(2,128)}, u32[]{:S(2)}) copy-start(f32[2,2048]{1,0:T(2,128)} %param.9) | copy-start | bytes 49156
  7.2 122.2 %all-gather.2.cloned.1.call-start = ((), (), s32[]{:S(2)}) async-start(), calls=%async_computation.1 | async-start | bytes 4718592 | tf_op jit(solution)/shard_map/all_gather | solution.py:33
  37.0 92.3 %copy-start.1 = (f32[2,1792]{1,0:T(2,128)}, f32[2,1792]{1,0:T(2,128)S(1)}, u32[]{:S(2)}) copy-start(f32[2,1792]{1,0:T(2,128)S(1)} %get-tuple-element.11) | copy-start | bytes 43012
  59.4 69.9 %copy-start = (f32[2,2048]{1,0:T(2,128)}, f32[2,2048]{1,0:T(2,128)S(1)}, u32[]{:S(2)}) copy-start(f32[2,2048]{1,0:T(2,128)S(1)} %add_multiply_fusion) | copy-start | bytes 49156
  71.0 327.4 %reduce-scatter.2.cloned.1.call-start = ((), (), s32[]{:S(2)}) async-start(), calls=%async_computation.2 | async-start | bytes 18350080 | tf_op jit(solution)/shard_map/reduce_scatter | solution.py:35
Sparse Core Ops, SparseCore 0:
  71.1 34.2 all-gather.1
  151.4 246.9 reduce-scatter.1
where the time goes:
time: 410 us; the launch traced here: 409 us
  waiting for transfers between devices  247 us (60%)
  blocking collectives  80.4 us (20%)
  other arithmetic  44.1 us (11%)
  matrix products  21.9 us (5%)
  between operations  14.1 us (3%)
    reduce_scatter x1, waiting for transfers between devices, local(): lax.psum_scatter(lax.dot_general(spread, flat_weights, (((1,), (1,)), (()...  247 us
    psum x1, blocking collectives, local(): norm_total = lax.psum(jnp.sum(update * update, axis=(1, 2)), ('row', 'col'))  37.5 us
    psum x1, blocking collectives, local(): row_mean = lax.psum(jnp.sum(row_new, axis=1), 'row') / FF  22.3 us
    dot_general x1, matrix products, local(): lax.dot_general(spread, flat_weights, (((1,), (1,)), ((), ())), preferred...  21.9 us
    convert_element_type x1, other arithmetic, local(): new_weights = (weights.astype(jnp.float32) - learn_rate * update / clip_s...  20.8 us
    psum x1, blocking collectives, local(): row_total = lax.psum(row_part, 'col')  20.5 us
    reduce_sum x1, other arithmetic, local(): norm_total = lax.psum(jnp.sum(update * update, axis=(1, 2)), ('row', 'col'))  11.5 us
    reduce_sum x1, other arithmetic, local(): col_part = jnp.sum(squares, axis=1)  9.13 us
  transfers between devices with their start and end apart: 2, of which 1 were waited for; matrix products, arithmetic and copies ran while one was open for 5% of the time, Pallas kernels for 0%

commit v1 on v0

--- a/solution.py
+++ b/solution.py
@@ -25,7 +25,7 @@
     row_mean = lax.psum(jnp.sum(row_new, axis=1), "row") / FF
     denominator = jnp.sqrt(row_new[:, :, None] * col_new[:, None, :] / row_mean[:, None, None])
     update = gradient / denominator
-    norm_total = lax.psum(jnp.sum(update * update, axis=(1, 2)), ("row", "col"))
+    norm_total = lax.psum(lax.psum(jnp.sum(update * update, axis=(1, 2)), "row"), "col")
     clip_scale = jnp.maximum(1.0, jnp.sqrt(norm_total / (FF * D)) / clip_limit)
     new_weights = (
         weights.astype(jnp.float32) - learn_rate * update / clip_scale[:, None, None]

time: 410 us -> 396 us (0.966)
  blocking collectives: 80.4 us -> 63.2 us
    psum x1 -> x2, blocking collectives: 37.5 us -> 20.3 us  [the longest x1 11.8 us: local(): lax.psum(jnp.sum(update * update, axis=(1, 2)), 'row')]
    all_gather x1, waiting for transfers between devices: 0.02 us -> 4.35 us  [local(): spread = lax.all_gather(tokens, 'row', axis=0, tiled=True)]
  transfers between devices with their start and end apart: 2 -> 2, of which waited for: 1 -> 2; matrix products, arithmetic and copies ran while one was open for 5% -> 5% of each run, Pallas kernels for 0% -> 0%
where the time goes in v1:
time: 396 us; the launch traced here: 395 us
  waiting for transfers between devices  250 us (63%)
  blocking collectives  63.2 us (16%)
  other arithmetic  44.4 us (11%)
  matrix products  21.9 us (6%)
  between operations  14.1 us (4%)
    reduce_scatter x1, waiting for transfers between devices, local(): lax.psum_scatter(lax.dot_general(spread, flat_weights, (((1,), (1,)), (()...  246 us
    psum x1, blocking collectives, local(): row_mean = lax.psum(jnp.sum(row_new, axis=1), 'row') / FF  22.3 us
    dot_general x1, matrix products, local(): lax.dot_general(spread, flat_weights, (((1,), (1,)), ((), ())), preferred...  21.9 us
    convert_element_type x1, other arithmetic, local(): new_weights = (weights.astype(jnp.float32) - learn_rate * update / clip_s...  21.1 us
    psum x1, blocking collectives, local(): row_total = lax.psum(row_part, 'col')  20.5 us
    psum x1, blocking collectives, local(): lax.psum(jnp.sum(update * update, axis=(1, 2)), 'row')  11.8 us
    reduce_sum x1, other arithmetic, local(): jnp.sum(update * update, axis=(1, 2))  11.5 us
    reduce_sum x1, other arithmetic, local(): col_part = jnp.sum(squares, axis=1)  9.13 us
  transfers between devices with their start and end apart: 2, of which 2 were waited for; matrix products, arithmetic and copies ran while one was open for 5% of the time, Pallas kernels for 0%

profile of v1, /device:TPU:0, one launch (start us, length us, event | category | flops | bytes accessed | tf_op | source)
XLA Modules:
  0.0 395.4 jit_solution(11339273190184058073)
XLA Ops:
  7.2 0.0 copy-start.3
  7.2 0.0 copy-start.2
  7.2 0.0 all-gather.2.cloned.1.call-start
  7.2 9.1 %fusion = (f32[2,2048]{1,0:T(2,128)S(1)}, f32[2,1792]{1,0:T(2,128)S(1)}) fusion(bf16[2,1792,2048]{2,1,0:T(8,128)(2,1)} %param.7), kind=kLoop, calls=%fused_computation.2 | loop fusion | flops 29352448 | bytes 14710784 | tf_op jit(solution)/shard_map/reduce_sum | solution.py:18
  16.4 20.5 %psum.35 = f32[2,1792]{1,0:T(2,128)S(1)} all-reduce(f32[2,1792]{1,0:T(2,128)S(1)} %get-tuple-element.7), channel_id=1, replica_groups=mesh['row'=8,'col'=4] {'col'}, use_global_device_ids=true, to_apply=%region_1.0 | all-reduce | flops 3584 | bytes 28672 | tf_op jit(solution)/shard_map/psum | solution.py:21
  36.9 0.0 copy-done.3
  36.9 0.1 fusion.3
  37.0 0.0 copy-start.1
  37.0 22.3 %all-reduce = (f32[2]{0:T(128)S(1)}, f32[2,2048]{1,0:T(2,128)S(1)}) all-reduce(f32[2]{0:T(128)S(1)} %get-tuple-element.10, f32[2,2048]{1,0:T(2,128)S(1)} %get-tuple-element.6), channel_id=1, replica_groups=mesh['row'=8,'col'=4] {'row'}, use_global_device_ids=true, to_apply=%region_5.0 | all-reduce | flops 4098 | bytes 32784 | tf_op jit(solution)/shard_map/psum | solution.py:25
  59.4 0.0 copy-done.2
  59.4 0.0 copy-start
  59.4 11.5 %multiply_reduce_fusion = f32[2]{0:T(128)S(1)} fusion(f32[2]{0:T(128)S(1)} %broadcast_multiply_fusion, f32[2,2048]{1,0:T(2,128)S(1)} %add_multiply_fusion, f32[2,1792]{1,0:T(2,128)S(1)} %get-tuple-element.11, bf16[2,1792,2048]{2,1,0:T(8,128)(2,1)} %param.7), kind=kLoop, calls=%fused_computation.5 | loop fusion | flops 44040192 | bytes 14710800 | tf_op jit(solution)/shard_map/reduce_sum | solution.py:28
  70.9 11.8 %psum.38 = f32[2]{0:T(128)S(1)} all-reduce(f32[2]{0:T(128)S(1)} %multiply_reduce_fusion), channel_id=1, replica_groups=mesh['row'=8,'col'=4] {'row'}, use_global_device_ids=true, to_apply=%region_7.0 | all-reduce | flops 2 | bytes 16 | tf_op jit(solution)/shard_map/psum | solution.py:28
  82.7 0.0 all-gather.2.cloned.1.call-update
  82.7 0.0 reduce-scatter.2.cloned.1.call-start
  82.8 8.6 %psum.39 = f32[2]{0:T(128)S(1)} all-reduce(f32[2]{0:T(128)S(1)} %psum.38), channel_id=1, replica_groups=mesh['row'=8,'col'=4] {'col'}, use_global_device_ids=true, to_apply=%region_8.0 | all-reduce | flops 2 | bytes 16 | tf_op jit(solution)/shard_map/psum | solution.py:28
  91.3 21.1 %subtract_convert_fusion = bf16[2,1792,2048]{2,1,0:T(8,128)(2,1)} fusion(bf16[2,1792,2048]{2,1,0:T(8,128)(2,1)} %param.6, f32[2]{0:T(128)S(1)} %sqrt_maximum_fusion, f32[2]{0:T(128)S(1)} %broadcast_multiply_fusion, f32[2,2048]{1,0:T(2,128)S(1)} %add_multiply_fusion, f32[2,1792]{1,0:T(2,128)S(1)} %get-tuple-element.11, bf16[2,1792,2048]{2,1,0:T(8,128)(2,1)} %param.7), kind=kLoop, calls=%fused_computation.4 | loop fusion | flops 66060288 | bytes 44070928 | tf_op jit(solution)/shard_map/convert_element_type | solution.py:32
  112.4 0.0 copy-done.1
  112.4 0.0 copy-done
  112.4 4.3 %all-gather.2.cloned.1.call-done = bf16[1024,2048]{1,0:T(8,128)(2,1)} async-done(((bf16[128,2048]{1,0:T(8,128)(2,1)}), bf16[1024,2048]{1,0:T(8,128)(2,1)}) %all-gather.2.cloned.1.call-update) | async-done | bytes 4194320 | tf_op jit(solution)/shard_map/all_gather | solution.py:33
  116.8 21.9 %convolution_bitcast_fusion = f32[1024,3584]{0,1:T(8,128)} fusion(bf16[3584,2048]{1,0:T(8,128)(2,1)} %bitcast.5, bf16[1024,2048]{1,0:T(8,128)(2,1)} %all-gather.2.cloned.1.call-done), kind=kOutput, calls=%fused_computation.6 | convolution fusion | flops 15032385536 | bytes 33554432 | tf_op jit(solution)/shard_map/dot_general | solution.py:36
  138.7 0.0 reduce-scatter.2.cloned.1.call-update
  138.7 245.9 %reduce-scatter.2.cloned.1.call-done = f32[256,3584]{0,1:T(8,128)} async-done(((f32[1024,3584]{0,1:T(8,128)}), f32[256,3584]{0,1:T(8,128)}) %reduce-scatter.2.cloned.1.call-update) | async-done | bytes 3670032 | tf_op jit(solution)/shard_map/reduce_scatter | solution.py:35
  384.6 2.6 fusion.2
  387.2 1.4 copy.8
  (3 shorter events, 0.0 us)
Async XLA Ops:
  7.2 29.7 %copy-start.3 = (f32[2,1792]{1,0:T(2,128)S(1)}, f32[2,1792]{1,0:T(2,128)}, u32[]{:S(2)}) copy-start(f32[2,1792]{1,0:T(2,128)} %param.8) | copy-start | bytes 43012
  7.2 52.2 %copy-start.2 = (f32[2,2048]{1,0:T(2,128)S(1)}, f32[2,2048]{1,0:T(2,128)}, u32[]{:S(2)}) copy-start(f32[2,2048]{1,0:T(2,128)} %param.9) | copy-start | bytes 49156
  7.2 109.6 %all-gather.2.cloned.1.call-start = ((), (), s32[]{:S(2)}) async-start(), calls=%async_computation.1 | async-start | bytes 4718592 | tf_op jit(solution)/shard_map/all_gather | solution.py:33
  37.0 75.4 %copy-start.1 = (f32[2,1792]{1,0:T(2,128)}, f32[2,1792]{1,0:T(2,128)S(1)}, u32[]{:S(2)}) copy-start(f32[2,1792]{1,0:T(2,128)S(1)} %get-tuple-element.11) | copy-start | bytes 43012
  59.4 53.0 %copy-start = (f32[2,2048]{1,0:T(2,128)}, f32[2,2048]{1,0:T(2,128)S(1)}, u32[]{:S(2)}) copy-start(f32[2,2048]{1,0:T(2,128)S(1)} %add_multiply_fusion) | copy-start | bytes 49156
  82.7 301.9 %reduce-scatter.2.cloned.1.call-start = ((), (), s32[]{:S(2)}) async-start(), calls=%async_computation.2 | async-start | bytes 18350080 | tf_op jit(solution)/shard_map/reduce_scatter | solution.py:35
Sparse Core Ops, SparseCore 0:
  82.8 33.8 all-gather.1
  138.8 245.7 reduce-scatter.1

commit v2 on v0

--- a/solution.py
+++ b/solution.py
@@ -25,7 +25,9 @@
     row_mean = lax.psum(jnp.sum(row_new, axis=1), "row") / FF
     denominator = jnp.sqrt(row_new[:, :, None] * col_new[:, None, :] / row_mean[:, None, None])
     update = gradient / denominator
-    norm_total = lax.psum(jnp.sum(update * update, axis=(1, 2)), ("row", "col"))
+    norm_total = jnp.sum(
+        lax.all_gather(jnp.sum(update * update, axis=(1, 2)), ("row", "col")), axis=0
+    )
     clip_scale = jnp.maximum(1.0, jnp.sqrt(norm_total / (FF * D)) / clip_limit)
     new_weights = (
         weights.astype(jnp.float32) - learn_rate * update / clip_scale[:, None, None]

time: 410 us -> 411 us (level)
    psum x1 -> x0, blocking collectives: 37.5 us -> none  [local(): norm_total = lax.psum(jnp.sum(update * update, axis=(1, 2)), ('row', 'col'))]
    unnamed x0 -> x1, blocking collectives: none -> 37.1 us
    reduce_sum x1 -> x2, other arithmetic: 11.5 us -> 11.5 us  [the longest x1 11.5 us: local(): jnp.sum(update * update, axis=(1, 2))]
  transfers between devices with their start and end apart: 2 -> 2, of which waited for: 1 -> 1; matrix products, arithmetic and copies ran while one was open for 5% -> 10% of each run, Pallas kernels for 0% -> 0%
where the time goes in v2:
time: 411 us; the launch traced here: 410 us
  waiting for transfers between devices  248 us (60%)
  blocking collectives  80.5 us (20%)
  other arithmetic  44.2 us (11%)
  matrix products  21.9 us (5%)
  between operations  14.1 us (3%)
    reduce_scatter x1, waiting for transfers between devices, local(): lax.psum_scatter(lax.dot_general(spread, flat_weights, (((1,), (1,)), (()...  247 us
    unnamed x1, blocking collectives  37.1 us
    psum x1, blocking collectives, local(): row_mean = lax.psum(jnp.sum(row_new, axis=1), 'row') / FF  22.9 us
    dot_general x1, matrix products, local(): lax.dot_general(spread, flat_weights, (((1,), (1,)), ((), ())), preferred...  21.9 us
    convert_element_type x1, other arithmetic, local(): new_weights = (weights.astype(jnp.float32) - learn_rate * update / clip_s...  20.8 us
    psum x1, blocking collectives, local(): row_total = lax.psum(row_part, 'col')  20.5 us
    reduce_sum x1, other arithmetic, local(): jnp.sum(update * update, axis=(1, 2))  11.5 us
    reduce_sum x1, other arithmetic, local(): col_part = jnp.sum(squares, axis=1)  9.13 us
  transfers between devices with their start and end apart: 2, of which 1 were waited for; matrix products, arithmetic and copies ran while one was open for 10% of the time, Pallas kernels for 0%

profile of v2, /device:TPU:0, one launch (start us, length us, event | category | flops | bytes accessed | tf_op | source)
XLA Modules:
  0.0 410.3 jit_solution(7428183282962463979)
XLA Ops:
  7.2 0.0 copy-start.3
  7.2 0.0 copy-start.2
  7.2 0.0 all-gather.3.cloned.1.call-start
  7.2 0.7 all-gather.3.cloned.1.call-update
  7.9 0.0 reduce-scatter.2.cloned.1.call-start
  8.0 9.1 %fusion = (f32[2,2048]{1,0:T(2,128)S(1)}, f32[2,1792]{1,0:T(2,128)S(1)}) fusion(bf16[2,1792,2048]{2,1,0:T(8,128)(2,1)} %param.7), kind=kLoop, calls=%fused_computation.2 | loop fusion | flops 29352448 | bytes 14710784 | tf_op jit(solution)/shard_map/reduce_sum | solution.py:18
  17.1 20.5 %psum.21 = f32[2,1792]{1,0:T(2,128)S(1)} all-reduce(f32[2,1792]{1,0:T(2,128)S(1)} %get-tuple-element.10), channel_id=1, replica_groups=mesh['row'=8,'col'=4] {'col'}, use_global_device_ids=true, to_apply=%region_1.0 | all-reduce | flops 3584 | bytes 28672 | tf_op jit(solution)/shard_map/psum | solution.py:21
  37.6 0.0 copy-done.3
  37.6 0.1 fusion.3
  37.8 0.0 copy-start.1
  37.8 22.9 %all-reduce.1 = (f32[2]{0:T(128)S(1)}, f32[2,2048]{1,0:T(2,128)S(1)}) all-reduce(f32[2]{0:T(128)S(1)} %get-tuple-element.13, f32[2,2048]{1,0:T(2,128)S(1)} %get-tuple-element.9), channel_id=1, replica_groups=mesh['row'=8,'col'=4] {'row'}, use_global_device_ids=true, to_apply=%region_5.0 | all-reduce | flops 4098 | bytes 32784 | tf_op jit(solution)/shard_map/psum | solution.py:25
  60.7 0.0 copy-done.2
  60.7 0.0 copy-start
  60.7 11.5 %multiply_reduce_fusion = f32[2]{0:T(128)S(1)} fusion(f32[2]{0:T(128)S(1)} %broadcast_multiply_fusion, f32[2,2048]{1,0:T(2,128)S(1)} %add_multiply_fusion, f32[2,1792]{1,0:T(2,128)S(1)} %get-tuple-element.14, bf16[2,1792,2048]{2,1,0:T(8,128)(2,1)} %param.7), kind=kLoop, calls=%fused_computation.5 | loop fusion | flops 44040192 | bytes 14710800 | tf_op jit(solution)/shard_map/reduce_sum | solution.py:29
  72.2 0.2 dynamic-update-slice
  72.4 37.1 %all-reduce = f32[64]{0:T(128)S(1)} all-reduce(f32[64]{0:T(128)S(1)} %dynamic-update-slice), channel_id=2, replica_groups=mesh['row'=8,'col'=4] {'row','col'}, use_global_device_ids=true, to_apply=%add | all-reduce | flops 64 | bytes 512
  109.5 0.1 reshape.18
  109.6 20.8 %subtract_convert_fusion = bf16[2,1792,2048]{2,1,0:T(8,128)(2,1)} fusion(bf16[2,1792,2048]{2,1,0:T(8,128)(2,1)} %param.6, f32[2]{0:T(128)S(1)} %sqrt_maximum_fusion, f32[2]{0:T(128)S(1)} %broadcast_multiply_fusion, f32[2,2048]{1,0:T(2,128)S(1)} %add_multiply_fusion, f32[2,1792]{1,0:T(2,128)S(1)} %get-tuple-element.14, bf16[2,1792,2048]{2,1,0:T(8,128)(2,1)} %param.7), kind=kLoop, calls=%fused_computation.4 | loop fusion | flops 66060288 | bytes 44070928 | tf_op jit(solution)/shard_map/convert_element_type | solution.py:34
  130.4 0.0 copy-done.1
  130.4 0.0 copy-done
  130.4 0.0 all-gather.3.cloned.1.call-done
  130.4 21.9 %convolution_bitcast_fusion = f32[1024,3584]{0,1:T(8,128)} fusion(bf16[3584,2048]{1,0:T(8,128)(2,1)} %bitcast.5, bf16[1024,2048]{1,0:T(8,128)(2,1)} %all-gather.3.cloned.1.call-done), kind=kOutput, calls=%fused_computation.6 | convolution fusion | flops 15032385536 | bytes 33554432 | tf_op jit(solution)/shard_map/dot_general | solution.py:38
  152.3 0.0 reduce-scatter.2.cloned.1.call-update
  152.3 247.2 %reduce-scatter.2.cloned.1.call-done = f32[256,3584]{0,1:T(8,128)} async-done(((f32[1024,3584]{0,1:T(8,128)}), f32[256,3584]{0,1:T(8,128)}) %reduce-scatter.2.cloned.1.call-update) | async-done | bytes 3670032 | tf_op jit(solution)/shard_map/reduce_scatter | solution.py:37
  399.5 2.6 fusion.2
  402.1 1.4 copy.9
  (5 shorter events, 0.1 us)
Async XLA Ops:
  7.2 30.5 %copy-start.3 = (f32[2,1792]{1,0:T(2,128)S(1)}, f32[2,1792]{1,0:T(2,128)}, u32[]{:S(2)}) copy-start(f32[2,1792]{1,0:T(2,128)} %param.8) | copy-start | bytes 43012
  7.2 53.5 %copy-start.2 = (f32[2,2048]{1,0:T(2,128)S(1)}, f32[2,2048]{1,0:T(2,128)}, u32[]{:S(2)}) copy-start(f32[2,2048]{1,0:T(2,128)} %param.9) | copy-start | bytes 49156
  7.2 123.2 %all-gather.3.cloned.1.call-start = ((), (), s32[]{:S(2)}) async-start(), calls=%async_computation.1 | async-start | bytes 4718592 | tf_op jit(solution)/shard_map/all_gather | solution.py:35
  7.9 391.6 %reduce-scatter.2.cloned.1.call-start = ((), (), s32[]{:S(2)}) async-start(), calls=%async_computation.2 | async-start | bytes 18350080 | tf_op jit(solution)/shard_map/reduce_scatter | solution.py:37
  37.8 92.6 %copy-start.1 = (f32[2,1792]{1,0:T(2,128)}, f32[2,1792]{1,0:T(2,128)S(1)}, u32[]{:S(2)}) copy-start(f32[2,1792]{1,0:T(2,128)S(1)} %get-tuple-element.14) | copy-start | bytes 43012
  60.7 69.7 %copy-start = (f32[2,2048]{1,0:T(2,128)}, f32[2,2048]{1,0:T(2,128)S(1)}, u32[]{:S(2)}) copy-start(f32[2,2048]{1,0:T(2,128)S(1)} %add_multiply_fusion) | copy-start | bytes 49156
Sparse Core Ops, SparseCore 0:
  9.9 39.3 all-gather.2
  152.5 247.0 reduce-scatter.1
